TPU v7x, 32 devices: a whole 2x2x4 slice. The times are simulated.
32 devices in a mesh: dp: 8 (over z, x), mp: 4 (over y, core).
Axes of the slice: x: 2, y: 2, z: 4, core: 2. Of those that a mesh axis runs over, the one named last changes fastest.
Arguments:
- z_star: bfloat16 [8, 257, 1280], P('dp', None, 'mp'), may hold values from -24 to 24
- cotangent: float32 [8, 257, 1280], P('dp', None, 'mp'), may hold values from -6 to 6
- w_qkv: bfloat16 [3, 1280, 1280], P(None, None, 'mp'), may hold values from -1 to 1
- w_out: bfloat16 [1280, 1280], P('mp'), may hold values from -0.15625 to 0.15625
Outputs:
- implicit: float32 [8, 257, 1280], P('dp', None, 'mp')
- grad_qkv: float32 [3, 1280, 1280], P(None, 'dp', 'mp')
- grad_out: float32 [1280, 1280], P('mp', 'dp')
All inputs are finite; a program needn't handle non-finite values.
Results may differ from a plain program's by a relative error of at most 0.0091.
Values may be sent and summed in bfloat16 or wider, within the bound.
A program may use at most 128 MiB of HBM per device.

v0:
```python
import math
import jax
import jax.numpy as jnp
from jax import lax
from jax.sharding import PartitionSpec as P

HD = 80
TERMS = 3
epsilon = 1e-06


def shards(z_star, cotangent, w_qkv, w_out):
    groups = lax.axis_size("mp")
    images, tokens, narrow = z_star.shape
    model_width = narrow * groups
    columns = w_qkv.shape[2]
    heads_here = columns // HD
    score_scale = HD ** (-0.5)
    position = lax.axis_index("mp")
    whole = lax.all_gather(z_star, "mp", axis=2, tiled=True)
    values = whole.astype(jnp.float32)
    centred = values - jnp.mean(values, axis=-1, keepdims=True)
    inv_std = lax.rsqrt(jnp.mean(centred * centred, axis=-1, keepdims=True) + epsilon)
    normal_f = centred * inv_std
    normal_b = normal_f.astype(jnp.bfloat16)
    flattened = normal_b.reshape(-1, model_width)

    def project(slot_index):
        result = jnp.dot(flattened, w_qkv[slot_index], preferred_element_type=jnp.float32)
        return result.astype(jnp.bfloat16).reshape(images, tokens, heads_here, HD)

    queries = project(0)
    key_vecs = project(1)
    val_vecs = project(2)
    scores = (
        jnp.einsum("bqhe,bkhe->bhqk", queries, key_vecs, preferred_element_type=jnp.float32)
        * score_scale
    )
    attn_probs = jax.nn.softmax(scores, axis=-1)
    probs_b = attn_probs.astype(jnp.bfloat16)
    attended = jnp.einsum("bhqk,bkhe->bqhe", probs_b, val_vecs, preferred_element_type=jnp.float32)
    attended = attended.astype(jnp.bfloat16).reshape(-1, columns)
    contract_first = (((0,), (0,)), ((), ()))
    contract_second = (((1,), (1,)), ((), ()))
    running = cotangent
    gathered = lax.all_gather(cotangent.astype(jnp.bfloat16), "mp", axis=2, tiled=True)
    cot_rows = gathered.reshape(-1, model_width)
    sum_q = None
    sum_o = None
    for term_index in range(TERMS):
        needs_input = term_index + 1 < TERMS
        att_grad = lax.dot_general(
            cot_rows, w_out, contract_second, preferred_element_type=jnp.float32
        )
        att_grad = att_grad.astype(jnp.bfloat16).reshape(images, tokens, heads_here, HD)
        grad_o = lax.dot_general(
            attended, cot_rows, contract_first, preferred_element_type=jnp.float32
        )
        prob_grad = jnp.einsum(
            "bqhe,bkhe->bhqk", att_grad, val_vecs, preferred_element_type=jnp.float32
        )
        rowdot = jnp.sum(attn_probs * prob_grad, axis=-1, keepdims=True)
        score_grad = (attn_probs * (prob_grad - rowdot) * score_scale).astype(jnp.bfloat16)
        q_grad = jnp.einsum(
            "bhqk,bkhe->bqhe", score_grad, key_vecs, preferred_element_type=jnp.float32
        ).astype(jnp.bfloat16)
        k_grad = jnp.einsum(
            "bhqk,bqhe->bkhe", score_grad, queries, preferred_element_type=jnp.float32
        ).astype(jnp.bfloat16)
        v_grad = jnp.einsum(
            "bhqk,bqhe->bkhe", probs_b, att_grad, preferred_element_type=jnp.float32
        ).astype(jnp.bfloat16)
        qkv_grads = [item.reshape(-1, columns) for item in (q_grad, k_grad, v_grad)]
        grad_q = jnp.stack(
            [
                lax.dot_general(flattened, item, contract_first, preferred_element_type=jnp.float32)
                for item in qkv_grads
            ]
        )
        in_part = None
        if needs_input:
            in_part = lax.dot_general(
                qkv_grads[0], w_qkv[0], contract_second, preferred_element_type=jnp.float32
            )
            in_part = in_part + lax.dot_general(
                qkv_grads[1], w_qkv[1], contract_second, preferred_element_type=jnp.float32
            )
            in_part = in_part + lax.dot_general(
                qkv_grads[2], w_qkv[2], contract_second, preferred_element_type=jnp.float32
            )
            in_part = in_part.reshape(images, tokens, model_width)
        grad_q, grad_o, in_part = (grad_q, grad_o, in_part)
        part_q, part_o = (grad_q, grad_o)
        if term_index == 0:
            sum_q, sum_o = (part_q, part_o)
        else:
            sum_q = sum_q + part_q
            sum_o = sum_o + part_o
        if needs_input:
            in_grad = lax.psum(in_part, "mp")
            row_mean = jnp.mean(in_grad, axis=-1, keepdims=True)
            row_dot = jnp.mean(in_grad * normal_f, axis=-1, keepdims=True)
            full_term = (in_grad - row_mean - normal_f * row_dot) * inv_std
            local_term, full_term = (
                lax.dynamic_slice_in_dim(full_term, position * narrow, narrow, 2),
                full_term,
            )
            running = running + local_term
            cot_rows = full_term.astype(jnp.bfloat16).reshape(-1, model_width)
    sum_q, sum_o = (
        lax.psum_scatter(sum_q, "dp", scatter_dimension=1, tiled=True),
        lax.psum_scatter(sum_o, "dp", scatter_dimension=1, tiled=True),
    )
    factor = 1.0 / math.sqrt(images * lax.axis_size("dp") * tokens)
    return (running, sum_q * factor, sum_o * factor)


def solution(mesh):
    return jax.shard_map(
        shards,
        mesh=mesh,
        in_specs=(P("dp", None, "mp"), P("dp", None, "mp"), P(None, None, "mp"), P("mp", None)),
        out_specs=(P("dp", None, "mp"), P(None, "dp", "mp"), P("mp", "dp")),
        check_vma=False,
    )
```

profile of v0, /device:TPU:0, one launch (start us, length us, event | category | flops | bytes accessed | tf_op | source)
XLA Modules:
  0.0 371.2 jit_solution(9127516188160858572)
XLA Ops:
  9.0 17.0 %all_gather.6 = bf16[1,257,1280]{1,0,2:T(2,128)(2,1)} all-gather(bf16[1,257,320]{1,0,2:T(2,128)(2,1)S(1)} %copy.102), channel_id=1, replica_groups=mesh['dp'=8,'mp'=4] {'mp'}, dimensions={2}, use_global_device_ids=true | all-gather | bytes 822400 | tf_op jit(solution)/shard_map/all_gather | solution.py:20
  26.0 3.8 %copy.103 = bf16[1,257,1280]{2,1,0:T(8,128)(2,1)S(1)} copy(bf16[1,257,1280]{1,0,2:T(2,128)(2,1)} %all_gather.6) | data formatting | bytes 1315840 | tf_op jit(solution)/shard_map/all_gather | solution.py:20
  30.3 2.0 convolution_convert_fusion.8
  36.2 15.6 %all_gather.7 = bf16[1,257,1280]{1,0,2:T(2,128)(2,1)} all-gather(bf16[1,257,320]{1,0,2:T(2,128)(2,1)S(1)} %copy.107), channel_id=1, replica_groups=mesh['dp'=8,'mp'=4] {'mp'}, dimensions={2}, use_global_device_ids=true | all-gather | bytes 822400 | tf_op jit(solution)/shard_map/all_gather | solution.py:46
  51.7 3.8 %copy.108 = bf16[1,257,1280]{2,1,0:T(8,128)(2,1)S(1)} copy(bf16[1,257,1280]{1,0,2:T(2,128)(2,1)} %all_gather.7) | data formatting | bytes 1315840 | tf_op jit(solution)/shard_map/all_gather | solution.py:46
  59.9 4.4 %fusion.65 = bf16[4,80,257]{2,1,0:T(8,128)(2,1)} fusion(bf16[257,4,80]{0,2,1:T(8,128)(2,1)S(1)} %bitcast.203, f32[4,257,257]{1,2,0:T(8,128)} %fusion.137, f32[4,257,257]{1,2,0:T(8,128)} %get-tuple-element.23, f32[4,257]{1,0:T(4,128)S(1)} %get-tuple-element.22), kind=kOutput, calls=%fused_computation.64 | convolution fusion | flops 44204256 | bytes 2446640 | tf_op jit(solution)/shard_map/bhqk,bqhe->bkhe/dot_general | solution.py:67
  64.3 4.5 %fusion.62 = bf16[4,80,257]{2,1,0:T(8,128)(2,1)} fusion(bf16[257,4,80]{0,2,1:T(8,128)(2,1)S(1)} %bitcast.208, f32[4,257,257]{1,2,0:T(8,128)} %fusion.137, f32[4,257,257]{1,2,0:T(8,128)} %get-tuple-element.23, f32[4,257]{1,0:T(4,128)S(1)} %get-tuple-element.22), kind=kOutput, calls=%fused_computation.63 | convolution fusion | flops 44204256 | bytes 2446640 | tf_op jit(solution)/shard_map/bhqk,bkhe->bqhe/dot_general | solution.py:64
  79.4 36.4 %all-reduce.3.cloned.1.call-done = f32[1,257,1280]{2,1,0:T(8,128)} async-done(((f32[1,257,1280]{2,1,0:T(8,128)}), f32[1,257,1280]{2,1,0:T(8,128)}) %all-reduce.3.cloned.1.call-update) | async-done | bytes 1315856 | tf_op jit(solution)/shard_map/psum | solution.py:100
  122.1 2.1 convolution_convert_fusion.2
  124.2 2.6 fusion.138
  126.8 4.6 %fusion.56 = bf16[4,80,257]{2,1,0:T(8,128)(2,1)} fusion(bf16[257,4,80]{0,2,1:T(8,128)(2,1)} %bitcast.206, f32[4,257,257]{1,2,0:T(8,128)} %fusion.138, f32[4,257,257]{1,2,0:T(8,128)} %get-tuple-element.23, f32[4,257]{1,0:T(4,128)S(1)} %get-tuple-element.22), kind=kOutput, calls=%fused_computation.61 | convolution fusion | flops 44204256 | bytes 2446640 | tf_op jit(solution)/shard_map/bhqk,bkhe->bqhe/dot_general | solution.py:64
  131.4 4.6 %fusion.59 = bf16[4,80,257]{2,1,0:T(8,128)(2,1)} fusion(bf16[257,4,80]{0,2,1:T(8,128)(2,1)} %bitcast.204, f32[4,257,257]{1,2,0:T(8,128)} %fusion.138, f32[4,257,257]{1,2,0:T(8,128)} %get-tuple-element.23, f32[4,257]{1,0:T(4,128)S(1)} %get-tuple-element.22), kind=kOutput, calls=%fused_computation.62 | convolution fusion | flops 44204256 | bytes 2446640 | tf_op jit(solution)/shard_map/bhqk,bqhe->bkhe/dot_general | solution.py:67
  139.7 2.8 fusion.6
  143.8 2.1 convolution_add_fusion.1
  145.9 36.5 %all-reduce.5.cloned.1.call-done = f32[1,257,1280]{2,1,0:T(8,128)} async-done(((f32[1,257,1280]{2,1,0:T(8,128)}), f32[1,257,1280]{2,1,0:T(8,128)}) %all-reduce.5.cloned.1.call-update) | async-done | bytes 1315856 | tf_op jit(solution)/shard_map/psum | solution.py:100
  186.3 2.1 convolution_add_fusion
  199.4 4.6 %fusion.50 = bf16[4,80,257]{2,1,0:T(8,128)(2,1)} fusion(bf16[257,4,80]{0,2,1:T(8,128)(2,1)S(1)} %bitcast.209, f32[4,257,257]{1,2,0:T(8,128)} %fusion.139, f32[4,257,257]{1,2,0:T(8,128)} %get-tuple-element.23, f32[4,257]{1,0:T(4,128)S(1)} %get-tuple-element.22), kind=kOutput, calls=%fused_computation.59 | convolution fusion | flops 44204256 | bytes 2446640 | tf_op jit(solution)/shard_map/bhqk,bkhe->bqhe/dot_general | solution.py:64
  204.0 2.9 convolution_bitcast_fusion.2
  206.9 3.9 %fusion.53 = bf16[4,80,257]{2,1,0:T(8,128)(2,1)S(1)} fusion(bf16[257,4,80]{0,2,1:T(8,128)(2,1)S(1)} %bitcast.205, f32[4,257,257]{1,2,0:T(8,128)} %fusion.139, f32[4,257,257]{1,2,0:T(8,128)} %get-tuple-element.23, f32[4,257]{1,0:T(4,128)S(1)} %get-tuple-element.22), kind=kOutput, calls=%fused_computation.60 | convolution fusion | flops 44204256 | bytes 2446640 | tf_op jit(solution)/shard_map/bhqk,bqhe->bkhe/dot_general | solution.py:67
  213.6 4.7 %fusion.4 = f32[3,1280,320]{1,2,0:T(8,128)} fusion(f32[1,1280,320]{1,2,0:T(8,128)S(1)} %copy-done.8, f32[1,1280,320]{1,2,0:T(8,128)S(1)} %copy-done.9, f32[1,1280,320]{1,2,0:T(8,128)S(1)} %copy-done.10, f32[1,1280,320]{1,2,0:T(8,128)} %convolution_bitcast_fusion.3, f32[1,1280,320]{1,2,0:T(8,128)} %convolution_bitcast_fusion.4, ...), kind=kLoop, calls=%fused_computation.5 | loop fusion | flops 9830400 | bytes 19660800 | tf_op jit(solution)/shard_map/add | solution.py:97
  218.3 9.1 %copy.136 = f32[3,1280,320]{2,0,1:T(4,128)} copy(f32[3,1280,320]{1,2,0:T(8,128)} %fusion.4) | data formatting | bytes 9830400
  227.4 10.4 %reshape.277 = f32[1280,960]{1,0:T(8,128)} reshape(f32[1280,3,320]{2,1,0:T(4,128)} %bitcast.174) | data formatting | bytes 9830400
  241.4 14.6 %reduce-scatter.5.cloned.1.call-done = f32[320,160]{0,1:T(8,128)} async-done(((f32[320,1280]{0,1:T(8,128)}), f32[320,160]{0,1:T(8,128)}) %reduce-scatter.5.cloned.1.call-update) | async-done | bytes 204816 | tf_op jit(solution)/shard_map/reduce_scatter | solution.py:112
  257.6 103.8 %reduce-scatter.7.cloned.1.call-done = f32[160,960]{1,0:T(8,128)} async-done(((f32[1280,960]{1,0:T(8,128)}), f32[160,960]{1,0:T(8,128)}) %reduce-scatter.7.cloned.1.call-update) | async-done | bytes 614416
  (119 shorter events, 58.3 us)
Async XLA Ops:
  7.2 48.4 %copy-start = (bf16[320,1280]{1,0:T(8,128)(2,1)S(1)}, bf16[320,1280]{1,0:T(8,128)(2,1)}, u32[]{:S(2)}) copy-start(bf16[320,1280]{1,0:T(8,128)(2,1)} %param.7) | copy-start | bytes 2457604
  7.2 108.6 %all-reduce.3.cloned.1.call-start = ((), (), s32[]{:S(2)}) async-start(), calls=%async_computation.2 | async-start | bytes 2703360 | tf_op jit(solution)/shard_map/psum | solution.py:100
  30.0 2.3 copy-start.5
  35.1 24.8 %copy-start.25 = (bf16[257,320]{0,1:T(8,128)(2,1)}, bf16[257,320]{0,1:T(8,128)(2,1)S(1)}, u32[]{:S(2)}) copy-start(bf16[257,320]{0,1:T(8,128)(2,1)S(1)} %copy.105) | copy-start | bytes 493444
  56.1 1.9 copy-start.27
  56.3 3.6 copy-start.15
  68.8 3.3 copy-start.6
  68.8 3.3 copy-start.18
  70.6 2.0 copy-start.23
  74.9 107.6 %all-reduce.5.cloned.1.call-start = ((), (), s32[]{:S(2)}) async-start(), calls=%async_computation.3 | async-start | bytes 2703360 | tf_op jit(solution)/shard_map/psum | solution.py:100
  75.1 1.9 copy-start.24
  115.8 1.9 copy-start.11
  142.4 113.5 %reduce-scatter.5.cloned.1.call-start = ((), (), s32[]{:S(2)}) async-start(), calls=%async_computation.4 | async-start | bytes 2211840 | tf_op jit(solution)/shard_map/reduce_scatter | solution.py:112
  182.5 1.9 copy-start.12
  184.3 1.9 copy-start.7
  188.4 2.8 copy-start.14
  188.4 173.0 %reduce-scatter.7.cloned.1.call-start = ((), (), s32[]{:S(2)}) async-start(), calls=%async_computation.5 | async-start | bytes 5898240
  191.2 1.9 copy-start.22
  193.1 1.9 copy-start.20
  195.1 1.9 copy-start.4
  197.5 1.9 copy-start.28
  204.0 2.9 copy-start.26
  210.8 1.9 copy-start.10
  211.5 2.0 copy-start.9
  (9 other events, 11.6 us)
Sparse Core Ops, SparseCore 0:
  75.0 40.6 all-reduce.2
  142.6 39.8 all-reduce.4
  188.5 67.4 reduce-scatter.4
  259.4 101.9 reduce-scatter.6
where the time goes:
time: 372 us; the launch traced here: 371 us
  waiting for transfers between devices  191 us (51%)
  matrix products  74.3 us (20%)
  local copies, waits for them, and re-layouts  43.4 us (12%)
  blocking collectives  32.5 us (9%)
  other arithmetic  14.8 us (4%)
  between operations  14.2 us (4%)
    unnamed x5, waiting for transfers between devices  104 us
    psum x2, waiting for transfers between devices, shards(): in_grad = lax.psum(in_part, 'mp')  72.9 us
    unnamed x66, local copies, waits for them, and re-layouts  31.6 us
    all_gather x1, blocking collectives, shards(): whole = lax.all_gather(z_star, 'mp', axis=2, tiled=True)  17 us
    dot_general x9, matrix products, shards(): lax.dot_general(flattened, item, contract_first, preferred_element_type=j...  15.8 us
    all_gather x1, blocking collectives, shards(): lax.all_gather(cotangent.astype(jnp.bfloat16), 'mp', axis=2, tiled=True)  15.6 us
    reduce_scatter x1, waiting for transfers between devices, shards(): lax.psum_scatter(sum_o, 'dp', scatter_dimension=1, tiled=True)  14.6 us
    dot_general x3, matrix products, shards(): jnp.einsum('bhqk,bkhe->bqhe', score_grad, key_vecs, preferred_element_typ...  13.7 us
  transfers between devices with their start and end apart: 4, of which 4 were waited for; matrix products, arithmetic and copies ran while one was open for 16% of the time, Pallas kernels for 0%

commit v1 on v0

--- a/solution.py
+++ b/solution.py
@@ -43,7 +43,7 @@
     contract_first = (((0,), (0,)), ((), ()))
     contract_second = (((1,), (1,)), ((), ()))
     running = cotangent
-    gathered = lax.all_gather(cotangent.astype(jnp.bfloat16), "mp", axis=2, tiled=True)
+    gathered = jnp.concatenate(lax.all_gather(cotangent.astype(jnp.bfloat16), "mp"), axis=2)
     cot_rows = gathered.reshape(-1, model_width)
     sum_q = None
     sum_o = None

time: 372 us -> 355 us (0.954)
  matrix products: 74.3 us -> 67.5 us
  blocking collectives: 32.5 us -> 25.8 us
  local copies, waits for them, and re-layouts: 43.4 us -> 38.3 us
    all_gather x1, blocking collectives: 15.6 us -> 8.86 us  [shards(): lax.all_gather(cotangent.astype(jnp.bfloat16), 'mp')]
    all_gather x1 -> x0, local copies, waits for them, and re-layouts: 3.79 us -> none  [shards(): lax.all_gather(cotangent.astype(jnp.bfloat16), 'mp', axis=2, tiled=True)]
    unnamed x66 -> x76, local copies, waits for them, and re-layouts: 31.6 us -> 32.1 us
where the time goes in v1:
time: 355 us; the launch traced here: 354 us
  waiting for transfers between devices  193 us (54%)
  matrix products  67.5 us (19%)
  local copies, waits for them, and re-layouts  38.3 us (11%)
  blocking collectives  25.8 us (7%)
  other arithmetic  14.8 us (4%)
  between operations  14.3 us (4%)
    unnamed x5, waiting for transfers between devices  104 us
    psum x2, waiting for transfers between devices, shards(): in_grad = lax.psum(in_part, 'mp')  73 us
    unnamed x76, local copies, waits for them, and re-layouts  32.1 us
    all_gather x1, blocking collectives, shards(): whole = lax.all_gather(z_star, 'mp', axis=2, tiled=True)  17 us
    reduce_scatter x1, waiting for transfers between devices, shards(): lax.psum_scatter(sum_o, 'dp', scatter_dimension=1, tiled=True)  16.3 us
    dot_general x9, matrix products, shards(): lax.dot_general(flattened, item, contract_first, preferred_element_type=j...  14.9 us
    dot_general x3, matrix products, shards(): jnp.einsum('bhqk,bqhe->bkhe', score_grad, queries, preferred_element_type...  11.5 us
    dot_general x3, matrix products, shards(): jnp.einsum('bhqk,bkhe->bqhe', score_grad, key_vecs, preferred_element_typ...  11.5 us
  transfers between devices with their start and end apart: 4, of which 4 were waited for; matrix products, arithmetic and copies ran while one was open for 16% of the time, Pallas kernels for 0%

profile of v1, /device:TPU:0, one launch (start us, length us, event | category | flops | bytes accessed | tf_op | source)
XLA Modules:
  0.0 354.4 jit_solution(11122001823822124913)
XLA Ops:
  9.0 17.0 %all_gather.9 = bf16[1,257,1280]{1,0,2:T(2,128)(2,1)} all-gather(bf16[1,257,320]{1,0,2:T(2,128)(2,1)S(1)} %copy.79), channel_id=1, replica_groups=mesh['dp'=8,'mp'=4] {'mp'}, dimensions={2}, use_global_device_ids=true | all-gather | bytes 822400 | tf_op jit(solution)/shard_map/all_gather | solution.py:20
  26.0 3.8 %copy.80 = bf16[1,257,1280]{2,1,0:T(8,128)(2,1)S(1)} copy(bf16[1,257,1280]{1,0,2:T(2,128)(2,1)} %all_gather.9) | data formatting | bytes 1315840 | tf_op jit(solution)/shard_map/all_gather | solution.py:20
  30.3 2.6 convolution_convert_fusion.8
  35.3 8.9 %all-gather = bf16[4,257,320]{2,1,0:T(8,128)(2,1)S(1)} all-gather(bf16[1,257,320]{2,1,0:T(8,128)(2,1)S(1)} %copy.116), channel_id=2, replica_groups=mesh['dp'=8,'mp'=4] {'mp'}, dimensions={0}, use_global_device_ids=true | all-gather | bytes 822400 | tf_op jit(solution)/shard_map/all_gather | solution.py:46
  50.9 3.8 %fusion.65 = bf16[4,80,257]{2,1,0:T(8,128)(2,1)S(1)} fusion(bf16[257,4,80]{0,2,1:T(8,128)(2,1)S(1)} %bitcast.204, f32[4,257,257]{1,2,0:T(8,128)} %fusion.134, f32[4,257,257]{1,2,0:T(8,128)} %get-tuple-element.20, f32[4,257]{1,0:T(4,128)S(1)} %get-tuple-element.19), kind=kOutput, calls=%fused_computation.64 | convolution fusion | flops 44204256 | bytes 2446640 | tf_op jit(solution)/shard_map/bhqk,bqhe->bkhe/dot_general | solution.py:67
  54.7 3.8 %fusion.62 = bf16[4,80,257]{2,1,0:T(8,128)(2,1)S(1)} fusion(bf16[257,4,80]{0,2,1:T(8,128)(2,1)S(1)} %bitcast.208, f32[4,257,257]{1,2,0:T(8,128)} %fusion.134, f32[4,257,257]{1,2,0:T(8,128)} %get-tuple-element.20, f32[4,257]{1,0:T(4,128)S(1)} %get-tuple-element.19), kind=kOutput, calls=%fused_computation.63 | convolution fusion | flops 44204256 | bytes 2446640 | tf_op jit(solution)/shard_map/bhqk,bkhe->bqhe/dot_general | solution.py:64
  65.7 1.9 convolution_bitcast_fusion.7
  68.1 36.4 %all-reduce.3.cloned.1.call-done = f32[1,257,1280]{2,1,0:T(8,128)} async-done(((f32[1,257,1280]{2,1,0:T(8,128)}), f32[1,257,1280]{2,1,0:T(8,128)}) %all-reduce.3.cloned.1.call-update) | async-done | bytes 1315856 | tf_op jit(solution)/shard_map/psum | solution.py:100
  111.4 3.8 %fusion.56 = bf16[4,80,257]{2,1,0:T(8,128)(2,1)S(1)} fusion(bf16[257,4,80]{0,2,1:T(8,128)(2,1)S(1)} %bitcast.209, f32[4,257,257]{1,2,0:T(8,128)} %fusion.135, f32[4,257,257]{1,2,0:T(8,128)} %get-tuple-element.20, f32[4,257]{1,0:T(4,128)S(1)} %get-tuple-element.19), kind=kOutput, calls=%fused_computation.61 | convolution fusion | flops 44204256 | bytes 2446640 | tf_op jit(solution)/shard_map/bhqk,bkhe->bqhe/dot_general | solution.py:64
  115.3 3.8 %fusion.59 = bf16[4,80,257]{2,1,0:T(8,128)(2,1)S(1)} fusion(bf16[257,4,80]{0,2,1:T(8,128)(2,1)S(1)} %bitcast.205, f32[4,257,257]{1,2,0:T(8,128)} %fusion.135, f32[4,257,257]{1,2,0:T(8,128)} %get-tuple-element.20, f32[4,257]{1,0:T(4,128)S(1)} %get-tuple-element.19), kind=kOutput, calls=%fused_computation.62 | convolution fusion | flops 44204256 | bytes 2446640 | tf_op jit(solution)/shard_map/bhqk,bqhe->bkhe/dot_general | solution.py:67
  122.7 2.8 fusion.6
  126.9 2.1 convolution_add_fusion.1
  129.0 36.5 %all-reduce.5.cloned.1.call-done = f32[1,257,1280]{2,1,0:T(8,128)} async-done(((f32[1,257,1280]{2,1,0:T(8,128)}), f32[1,257,1280]{2,1,0:T(8,128)}) %all-reduce.5.cloned.1.call-update) | async-done | bytes 1315856 | tf_op jit(solution)/shard_map/psum | solution.py:100
  169.4 2.1 convolution_add_fusion
  174.3 1.9 convolution_bitcast_fusion.3
  176.2 1.9 convolution_bitcast_fusion.4
  178.2 1.9 convolution_bitcast_fusion.5
  182.5 3.9 %fusion.50 = bf16[4,80,257]{2,1,0:T(8,128)(2,1)S(1)} fusion(bf16[257,4,80]{0,2,1:T(8,128)(2,1)S(1)} %bitcast.210, f32[4,257,257]{1,2,0:T(8,128)} %fusion.136, f32[4,257,257]{1,2,0:T(8,128)} %get-tuple-element.20, f32[4,257]{1,0:T(4,128)S(1)} %get-tuple-element.19), kind=kOutput, calls=%fused_computation.59 | convolution fusion | flops 44204256 | bytes 2446640 | tf_op jit(solution)/shard_map/bhqk,bkhe->bqhe/dot_general | solution.py:64
  188.3 3.9 %fusion.53 = bf16[4,80,257]{2,1,0:T(8,128)(2,1)S(1)} fusion(bf16[257,4,80]{0,2,1:T(8,128)(2,1)S(1)} %bitcast.206, f32[4,257,257]{1,2,0:T(8,128)} %fusion.136, f32[4,257,257]{1,2,0:T(8,128)} %get-tuple-element.20, f32[4,257]{1,0:T(4,128)S(1)} %get-tuple-element.19), kind=kOutput, calls=%fused_computation.60 | convolution fusion | flops 44204256 | bytes 2446640 | tf_op jit(solution)/shard_map/bhqk,bqhe->bkhe/dot_general | solution.py:67
  195.1 4.7 %fusion.4 = f32[3,1280,320]{1,2,0:T(8,128)} fusion(f32[1,1280,320]{1,2,0:T(8,128)S(1)} %copy-done.8, f32[1,1280,320]{1,2,0:T(8,128)S(1)} %copy-done.9, f32[1,1280,320]{1,2,0:T(8,128)S(1)} %copy-done.10, f32[1,1280,320]{1,2,0:T(8,128)} %convolution_bitcast_fusion.3, f32[1,1280,320]{1,2,0:T(8,128)} %convolution_bitcast_fusion.4, ...), kind=kLoop, calls=%fused_computation.5 | loop fusion | flops 9830400 | bytes 19660800 | tf_op jit(solution)/shard_map/add | solution.py:97
  199.8 9.1 %copy.112 = f32[3,1280,320]{2,0,1:T(4,128)} copy(f32[3,1280,320]{1,2,0:T(8,128)} %fusion.4) | data formatting | bytes 9830400
  208.9 10.4 %reshape.278 = f32[1280,960]{1,0:T(8,128)} reshape(f32[1280,3,320]{2,1,0:T(4,128)} %bitcast.174) | data formatting | bytes 9830400
  222.9 16.3 %reduce-scatter.5.cloned.1.call-done = f32[320,160]{0,1:T(8,128)} async-done(((f32[320,1280]{0,1:T(8,128)}), f32[320,160]{0,1:T(8,128)}) %reduce-scatter.5.cloned.1.call-update) | async-done | bytes 204816 | tf_op jit(solution)/shard_map/reduce_scatter | solution.py:112
  240.9 103.7 %reduce-scatter.7.cloned.1.call-done = f32[160,960]{1,0:T(8,128)} async-done(((f32[1280,960]{1,0:T(8,128)}), f32[160,960]{1,0:T(8,128)}) %reduce-scatter.7.cloned.1.call-update) | async-done | bytes 614416
  (129 shorter events, 52.9 us)
Async XLA Ops:
  7.2 38.4 %copy-start = (bf16[320,1280]{1,0:T(8,128)(2,1)S(1)}, bf16[320,1280]{1,0:T(8,128)(2,1)}, u32[]{:S(2)}) copy-start(bf16[320,1280]{1,0:T(8,128)(2,1)} %param.7) | copy-start | bytes 2457604
  7.2 97.3 %all-reduce.3.cloned.1.call-start = ((), (), s32[]{:S(2)}) async-start(), calls=%async_computation.2 | async-start | bytes 2703360 | tf_op jit(solution)/shard_map/psum | solution.py:100
  30.0 3.0 copy-start.5
  46.9 4.0 %copy-start.25 = (bf16[257,320]{0,1:T(8,128)(2,1)}, bf16[257,320]{0,1:T(8,128)(2,1)S(1)}, u32[]{:S(2)}) copy-start(bf16[257,320]{0,1:T(8,128)(2,1)S(1)} %copy.82) | copy-start | bytes 493444
  47.3 3.6 %copy-start.28 = (bf16[257,320]{0,1:T(8,128)(2,1)}, bf16[257,320]{0,1:T(8,128)(2,1)S(1)}, u32[]{:S(2)}) copy-start(bf16[257,320]{0,1:T(8,128)(2,1)S(1)} %copy.81) | copy-start | bytes 493444
  50.9 3.8 %copy-start.29 = (bf16[257,320]{0,1:T(8,128)(2,1)S(1)}, bf16[257,320]{0,1:T(8,128)(2,1)}, u32[]{:S(2)}) copy-start(bf16[257,320]{0,1:T(8,128)(2,1)} %copy-done.28) | copy-start | bytes 493444
  58.5 2.3 copy-start.19
  58.5 2.3 copy-start.6
  63.6 101.9 %all-reduce.5.cloned.1.call-start = ((), (), s32[]{:S(2)}) async-start(), calls=%async_computation.3 | async-start | bytes 2703360 | tf_op jit(solution)/shard_map/psum | solution.py:100
  108.6 2.8 copy-start.30
  111.4 3.8 %copy-start.26 = (bf16[257,320]{0,1:T(8,128)(2,1)S(1)}, bf16[257,320]{0,1:T(8,128)(2,1)}, u32[]{:S(2)}) copy-start(bf16[257,320]{0,1:T(8,128)(2,1)} %copy-done.25) | copy-start | bytes 493444
  115.2 3.9 %copy-start.21 = (bf16[4,80,257]{2,1,0:T(8,128)(2,1)}, bf16[4,80,257]{2,1,0:T(8,128)(2,1)S(1)}, u32[]{:S(2)}) copy-start(bf16[4,80,257]{2,1,0:T(8,128)(2,1)S(1)} %fusion.56) | copy-start | bytes 493444
  119.1 3.5 copy-start.23
  122.6 2.9 copy-start.14
  125.5 113.7 %reduce-scatter.5.cloned.1.call-start = ((), (), s32[]{:S(2)}) async-start(), calls=%async_computation.4 | async-start | bytes 2211840 | tf_op jit(solution)/shard_map/reduce_scatter | solution.py:112
  167.4 1.9 copy-start.7
  171.5 2.8 copy-start.16
  171.5 173.1 %reduce-scatter.7.cloned.1.call-start = ((), (), s32[]{:S(2)}) async-start(), calls=%async_computation.5 | async-start | bytes 5898240
  174.3 1.9 copy-start.24
  176.2 2.0 copy-start.22
  178.2 1.9 copy-start.4
  186.4 1.9 copy-start.27
  192.2 1.9 copy-start.10
  193.0 2.1 copy-start.9
  (14 other events, 19.7 us)
Sparse Core Ops, SparseCore 0:
  63.7 40.7 all-reduce.2
  125.6 39.8 all-reduce.4
  171.6 67.5 reduce-scatter.4
  242.7 101.8 reduce-scatter.6
